TPU v7x, 128 devices: a whole 4x4x4 slice. The times are simulated.
128 devices in a mesh: freq: 4 (over y), pts: 32 (over z, x, core).
Axes of the slice: x: 4, y: 4, z: 4, core: 2. Of those that a mesh axis runs over, the one named last changes fastest.
Arguments:
- data: float32 [2, 32, 64, 3, 32768], P(None, 'freq', None, None, 'pts'), may hold values from -180 to 180
- quad_weight: float32 [32768], P('pts'), may hold values from 0.2 to 5
- basis: float32 [2, 32, 64, 8], P(None, 'freq'), may hold values from -6 to 6
Outputs:
- basis_out: float32 [2, 32, 64, 8], P(None, 'freq')
- spectrum: float32 [32, 8], P('freq')
- modes: float32 [2, 32, 8, 3, 32768], P(None, 'freq', None, None, 'pts')
All inputs are finite; a program needn't handle non-finite values.
Results may differ from a plain program's by a relative error of at most 0.0001.
Values sent between devices are 32-bit elements; how exact they have to be, the bound alone decides.
No kernel may reach another device: no remote copies, remote signals or barrier semaphores. Data moves between devices by JAX's collectives and lax.ppermute only.
A program may use at most 128 MiB of HBM per device.

v0:
```python
import jax
import jax.numpy as jnp
from jax import lax
from jax.experimental import pallas as pl
from jax.experimental.pallas import tpu as pltpu
from jax.sharding import PartitionSpec as P

ITERS = 4
F32 = jnp.float32
BF16 = jnp.bfloat16


def split(x):
    high = x.astype(BF16)
    low = (x - high.astype(F32)).astype(BF16)
    return high, low


def dot_rows(left, right):
    return lax.dot_general(left, right, (((1,), (1,)), ((), ())), preferred_element_type=F32)


def dot_plain(left, right):
    return lax.dot_general(left, right, (((1,), (0,)), ((), ())), preferred_element_type=F32)


def gram_kernel(freqs, blocks, comps, scaling, data, weight, out, buf, sems):
    copies = [
        pltpu.make_async_copy(data.at[:, f], buf.at[f], sems.at[f]) for f in range(freqs)
    ]
    for copy in copies:
        copy.start()
    root = jnp.sqrt(weight[...])
    row = lax.broadcasted_iota(jnp.int32, (blocks, blocks), 0)
    col = lax.broadcasted_iota(jnp.int32, (blocks, blocks), 1)
    both = 2 * blocks
    trace = jnp.zeros((blocks, blocks), F32)
    for pair in range(freqs // 2):
        packed = []
        for f in (2 * pair, 2 * pair + 1):
            copies[f].wait()
            acc = jnp.zeros((both, 2 * both), F32)
            for c in range(comps):
                x = buf[f, :, c].reshape(both, -1) * root
                high, low = split(x)
                acc = acc + dot_rows(high, jnp.concatenate([high, low], axis=0))
            cross = acc[:, both:]
            full = (acc[:, :both] + (cross + cross.T)) * scaling
            real = full[:blocks, :blocks] + full[blocks:, blocks:]
            imag = full[:blocks, blocks:] - full[blocks:, :blocks]
            packed.append(jnp.where(row <= col, real, imag))
            trace = trace + jnp.where(row == col, real, 0.0)
        wide = jnp.concatenate(packed, axis=1)
        for b in range(blocks // 8):
            start = (pair * (blocks // 8) + b) * 9
            out[start : start + 8, 0, :] = wide[8 * b : 8 * b + 8, :]
    value = jnp.sum(jnp.sum(trace, axis=1, keepdims=True), axis=0, keepdims=True)
    line = jnp.broadcast_to(value, (1, both))
    for piece in range(freqs // 2 * blocks // 8):
        out[piece * 9 + 8, 0:1, :] = line


def sum_kernel(pieces, arrived, out, trace):
    total = arrived[0:8, 0, :]
    line = arrived[8, 0:1, :]
    for p in range(1, pieces):
        total = total + arrived[9 * p : 9 * p + 8, 0, :]
        line = line + arrived[9 * p + 8, 0:1, :]
    for p in range(pieces):
        out[p] = total
    trace[...] = line


def finish_kernel(freqs, blocks, comps, rank, gram, basis, data, vec_out, ray_out, modes, buf, res, sems, out_sems):
    reads = [pltpu.make_async_copy(data.at[:, f], buf.at[f], sems.at[f]) for f in range(freqs)]
    for copy in reads:
        copy.start()
    both = 2 * blocks
    row = lax.broadcasted_iota(jnp.int32, (blocks, blocks), 0)
    col = lax.broadcasted_iota(jnp.int32, (blocks, blocks), 1)
    mats = []
    for f in range(freqs):
        packed = gram[f // 2][:, (f % 2) * blocks : (f % 2 + 1) * blocks]
        flipped = packed.T
        real = jnp.where(row <= col, packed, flipped)
        imag = jnp.where(row > col, packed, jnp.where(row < col, -flipped, 0.0))
        top = jnp.concatenate([real, -imag], axis=1)
        bottom = jnp.concatenate([imag, real], axis=1)
        high, low = split(jnp.concatenate([top, bottom], axis=0))
        mats.append(jnp.concatenate([high, low], axis=1))

    def apply(vec):
        parts = []
        for f in range(freqs):
            high, low = split(vec[f])
            out = dot_plain(jnp.concatenate([high, low], axis=0), mats[f])
            out = out[:rank] + out[rank:]
            parts.append((out[:, both:] + out[:, :both])[None])
        return jnp.concatenate(parts, axis=0)

    lane = lax.broadcasted_iota(jnp.int32, (1, 1, both), 2)
    sub = lax.broadcasted_iota(jnp.int32, (1, rank, 1), 1)
    sign = jnp.where(lane < blocks, -1.0, 1.0).astype(F32)

    def orthonormalize(z):
        for k in range(rank):
            base = z[:, k : k + 1, :]
            turned = pltpu.roll(base.reshape(freqs, both), blocks, 1).reshape(freqs, 1, both) * sign
            norm = jnp.sum(base * base, axis=2, keepdims=True) * (1.0 / blocks) + 1e-6
            factor = lax.rsqrt(norm)
            if k + 1 < rank:
                dot_real = jnp.sum(base * z, axis=2, keepdims=True)
                dot_imag = jnp.sum(turned * z, axis=2, keepdims=True)
                square = factor * factor * (1.0 / blocks)
                moved = z - (dot_real * square) * base - (dot_imag * square) * turned
            else:
                moved = z
            z = jnp.where(sub == k, z * factor, jnp.where(sub > k, moved, z))
        return z

    vec = jnp.concatenate([basis[0], basis[1]], axis=2)
    for step in range(ITERS):
        vec = orthonormalize(apply(vec))
    z = apply(vec)
    ray = jnp.sum(vec * z, axis=2, keepdims=True) * (1.0 / blocks)
    ray_out[...] = jnp.sum(jnp.where(sub == lane, ray, 0.0), axis=1)[:, :rank]
    vec_out[0] = vec[:, :, :blocks]
    vec_out[1] = vec[:, :, blocks:]

    writes = []
    for f in range(freqs):
        reads[f].wait()
        v = vec[f] * (1.0 / blocks)
        real_row = jnp.where(lane[0] < blocks, v, -v)
        imag_row = pltpu.roll(v, blocks, 1)
        high, low = split(jnp.concatenate([real_row, imag_row], axis=0))
        coef = jnp.concatenate(
            [jnp.concatenate([high, high], axis=1), jnp.concatenate([low, jnp.zeros_like(low)], axis=1)], axis=0
        )
        for c in range(comps):
            x = buf[f, :, c].reshape(both, -1)
            x_high, x_low = split(x)
            out = dot_plain(coef, jnp.concatenate([x_high, x_low], axis=0))
            out = out[: 2 * rank] + out[2 * rank :]
            res[0, f, c] = out[:rank]
            res[1, f, c] = out[rank:]
        copy = pltpu.make_async_copy(res.at[:, f], modes.at[:, f], out_sems.at[f])
        copy.start()
        writes.append(copy)
    for copy in writes:
        copy.wait()


def per_device(data, quad_weight, basis):
    _, freqs, blocks, comps, points = data.shape
    rank = basis.shape[-1]
    freq_groups = lax.axis_size("freq")
    size = lax.axis_size("pts")
    freq_count = freqs * freq_groups
    scaling = 1.0 / (comps * points * size)
    pieces = freqs // 2 * blocks // 8
    samples = jnp.transpose(data, (0, 1, 3, 2, 4))
    start = jnp.transpose(basis, (0, 1, 3, 2))
    vmem = pl.BlockSpec(memory_space=pltpu.VMEM)
    hbm = pl.BlockSpec(memory_space=pltpu.MemorySpace.HBM)
    packed = pl.pallas_call(
        lambda *refs: gram_kernel(freqs, blocks, comps, scaling, *refs),
        out_shape=jax.ShapeDtypeStruct((pieces * 9, 1, 2 * blocks), F32),
        in_specs=[hbm, vmem],
        out_specs=vmem,
        scratch_shapes=[
            pltpu.VMEM((freqs, 2, comps, blocks, points), F32),
            pltpu.SemaphoreType.DMA((freqs,)),
        ],
        compiler_params=pltpu.CompilerParams(vmem_limit_bytes=60 * 2**20),
        name="gram",
    )(samples, quad_weight.reshape(1, points))
    arrived = lax.all_to_all(packed, "pts", 0, 0, tiled=True)
    spread, trace = pl.pallas_call(
        lambda *refs: sum_kernel(size, *refs),
        out_shape=(
            jax.ShapeDtypeStruct((size, 8, 2 * blocks), F32),
            jax.ShapeDtypeStruct((1, 2 * blocks), F32),
        ),
        in_specs=[vmem],
        out_specs=(vmem, vmem),
        compiler_params=pltpu.CompilerParams(vmem_limit_bytes=2 * 2**20),
        name="total",
    )(arrived)
    trace = trace + lax.ppermute(trace, "freq", [(i, i ^ 1) for i in range(freq_groups)])
    gram = lax.all_to_all(spread, "pts", 0, 0, tiled=True).reshape(freqs // 2, blocks, 2 * blocks)
    gram, trace = lax.optimization_barrier((gram, trace))
    other = lax.ppermute(trace, "freq", [(i, i ^ 2) for i in range(freq_groups)])
    vec, ray, modes = pl.pallas_call(
        lambda *refs: finish_kernel(freqs, blocks, comps, rank, *refs),
        out_shape=(
            jax.ShapeDtypeStruct((2, freqs, rank, blocks), F32),
            jax.ShapeDtypeStruct((freqs, rank), F32),
            jax.ShapeDtypeStruct((2, freqs, comps, rank, points), F32),
        ),
        in_specs=[vmem, vmem, hbm],
        out_specs=(vmem, vmem, hbm),
        scratch_shapes=[
            pltpu.VMEM((freqs, 2, comps, blocks, points), F32),
            pltpu.VMEM((2, freqs, comps, rank, points), F32),
            pltpu.SemaphoreType.DMA((freqs,)),
            pltpu.SemaphoreType.DMA((freqs,)),
        ],
        compiler_params=pltpu.CompilerParams(vmem_limit_bytes=60 * 2**20),
        name="finish",
    )(gram, start, samples)
    total = (trace + other)[0, 0]
    spectrum = ray * (freq_count * blocks) / total
    return (
        jnp.transpose(vec, (0, 1, 3, 2)),
        spectrum,
        jnp.transpose(modes, (0, 1, 3, 2, 4)),
    )


def solution(mesh):
    in_specs = (P(None, "freq", None, None, "pts"), P("pts"), P(None, "freq", None, None))
    out_specs = (P(None, "freq", None, None), P("freq", None), P(None, "freq", None, None, "pts"))
    return jax.shard_map(
        per_device, mesh=mesh, in_specs=in_specs, out_specs=out_specs, check_vma=False
    )
```

profile of v0, /device:TPU:1, one launch (start us, length us, event | category | flops | bytes accessed | tf_op | source)
XLA Modules:
  0.0 59.2 jit_solution(11364520554276774206)
XLA Ops:
  0.6 12.8 %gram.1 = f32[288,1,128]{2,1,0:T(1,128)} custom-call(f32[2,8,3,64,1024]{4,3,2,1,0:T(8,128)} %bitcast.8, f32[1,1024]{1,0:T(1,128)} %bitcast.12), custom_call_target="tpu_custom_call" | custom-call | tf_op jit(solution)/shard_map/gram/pallas_call | solution.py:166
  13.4 17.2 %all_to_all.10.refs_0_ = f32[288,1,128]{2,1,0:T(1,128)S(1)} all-to-all(f32[288,1,128]{2,1,0:T(1,128)} %gram.1), channel_id=1, replica_groups=mesh['freq'=4,'pts'=32] {'pts'}, dimensions={0} | all-to-all | bytes 294912 | tf_op jit(solution)/shard_map/all_to_all | solution.py:178
  30.6 0.7 %total.1 = (f32[32,8,128]{2,1,0:T(8,128)}, f32[1,128]{1,0:T(1,128)S(1)}) custom-call(f32[288,1,128]{2,1,0:T(1,128)S(1)} %all_to_all.10.refs_0_), custom_call_target="tpu_custom_call" | custom-call | tf_op jit(solution)/shard_map/total/pallas_call | solution.py:179
  31.3 3.9 %all-to-all-start.1 = ((f32[32,8,128]{2,1,0:T(8,128)}), f32[32,8,128]{2,1,0:T(8,128)S(1)}, u32[]{:S(2)}, u32[]{:S(2)}) async-start(f32[32,8,128]{2,1,0:T(8,128)} %get-tuple-element.10), calls=%async_computation.1 | async-start | bytes 262144 | tf_op jit(solution)/shard_map/all_to_all | solution.py:191
  35.2 1.4 %collective-permute-start = (f32[1,128]{1,0:T(1,128)S(1)}, f32[1,128]{1,0:T(1,128)S(1)}, u32[]{:S(2)}, u32[]{:S(2)}) collective-permute-start(f32[1,128]{1,0:T(1,128)S(1)} %get-tuple-element.11), channel_id=1, source_target_pairs={{0,32},{32,0},{64,96},{96,64},{1,33},{33,1},{65,97},{97,65},{2,34}... | collective-permute-start | bytes 1544 | tf_op jit(solution)/shard_map/ppermute | solution.py:190
  36.6 1.4 %collective-permute-done = f32[1,128]{1,0:T(1,128)S(1)} collective-permute-done((f32[1,128]{1,0:T(1,128)S(1)}, f32[1,128]{1,0:T(1,128)S(1)}, u32[]{:S(2)}, u32[]{:S(2)}) %collective-permute-start) | collective-permute-done | bytes 544 | tf_op jit(solution)/shard_map/ppermute | solution.py:190
  38.0 5.0 %all-to-all-done.1 = f32[32,8,128]{2,1,0:T(8,128)S(1)} async-done(((f32[32,8,128]{2,1,0:T(8,128)}), f32[32,8,128]{2,1,0:T(8,128)S(1)}, u32[]{:S(2)}, u32[]{:S(2)}) %all-to-all-start.1) | async-done | bytes 131104 | tf_op jit(solution)/shard_map/all_to_all | solution.py:191
  42.9 0.0 copy-start
  42.9 2.9 %collective-permute-start.1 = (f32[1,128]{1,0:T(1,128)S(1)}, f32[1,128]{1,0:T(1,128)S(1)}, u32[]{:S(2)}, u32[]{:S(2)}) collective-permute-start(f32[1,128]{1,0:T(1,128)S(1)} %add.6), channel_id=1, source_target_pairs={{0,64},{32,96},{64,0},{96,32},{1,65},{33,97},{65,1},{97,33},{2,66}... | collective-permute-start | bytes 1544 | tf_op jit(solution)/shard_map/ppermute | solution.py:193
  45.9 0.0 copy-done
  45.9 12.0 %finish.1 = (f32[2,8,8,64]{3,2,1,0:T(8,128)}, f32[8,8]{1,0:T(8,128)}, f32[2,8,3,8,1024]{4,3,2,1,0:T(8,128)}) custom-call(f32[4,64,128]{2,1,0:T(8,128)} %bitcast.10, f32[2,8,8,64]{3,2,1,0:T(8,128)} %bitcast.11, f32[2,8,3,64,1024]{4,3,2,1,0:T(8,128)} %bitcast.9), custom_call_target="tpu_custom_call" | custom-call | tf_op jit(solution)/shard_map/finish/pallas_call | solution.py:194
  57.9 0.0 collective-permute-done.1
  57.9 1.3 %multiply_divide_fusion = f32[8,8]{1,0:T(8,128)} fusion(f32[8,8]{1,0:T(8,128)} %get-tuple-element.14, f32[]{:T(128)S(1)} %bitcast.13), kind=kLoop, calls=%fused_computation | loop fusion | flops 128 | bytes 516 | tf_op jit(solution)/shard_map/div | solution.py:213
  (2 shorter events, 0.0 us)
Async XLA Ops:
  31.3 11.6 %all-to-all-start.1 = ((f32[32,8,128]{2,1,0:T(8,128)}), f32[32,8,128]{2,1,0:T(8,128)S(1)}, u32[]{:S(2)}, u32[]{:S(2)}) async-start(f32[32,8,128]{2,1,0:T(8,128)} %get-tuple-element.10), calls=%async_computation.1 | async-start | bytes 262144 | tf_op jit(solution)/shard_map/all_to_all | solution.py:191
  35.2 2.7 %collective-permute-start = (f32[1,128]{1,0:T(1,128)S(1)}, f32[1,128]{1,0:T(1,128)S(1)}, u32[]{:S(2)}, u32[]{:S(2)}) collective-permute-start(f32[1,128]{1,0:T(1,128)S(1)} %get-tuple-element.11), channel_id=1, source_target_pairs={{0,32},{32,0},{64,96},{96,64},{1,33},{33,1},{65,97},{97,65},{2,34}... | collective-permute-start | bytes 1544 | tf_op jit(solution)/shard_map/ppermute | solution.py:190
  42.9 2.9 %copy-start = (f32[32,8,128]{2,1,0:T(8,128)}, f32[32,8,128]{2,1,0:T(8,128)S(1)}, u32[]{:S(2)}) copy-start(f32[32,8,128]{2,1,0:T(8,128)S(1)} %all-to-all-done.1) | copy-start | bytes 393220
  42.9 14.9 %collective-permute-start.1 = (f32[1,128]{1,0:T(1,128)S(1)}, f32[1,128]{1,0:T(1,128)S(1)}, u32[]{:S(2)}, u32[]{:S(2)}) collective-permute-start(f32[1,128]{1,0:T(1,128)S(1)} %add.6), channel_id=1, source_target_pairs={{0,64},{32,96},{64,0},{96,32},{1,65},{33,97},{65,1},{97,33},{2,66}... | collective-permute-start | bytes 1544 | tf_op jit(solution)/shard_map/ppermute | solution.py:193
where the time goes:
time: 59.5 us; the launch traced here: 59.2 us
  Pallas kernels  25.5 us (43%)
  blocking collectives  17.2 us (29%)
  starting transfers between devices  8.19 us (14%)
  waiting for transfers between devices  6.33 us (11%)
  other arithmetic  1.33 us (2%)
  between operations  0.67 us (1%)
    all_to_all x1, blocking collectives, per_device(): arrived = lax.all_to_all(packed, 'pts', 0, 0, tiled=True)  17.2 us
    pallas_call x1, Pallas kernels, per_device(): pl.pallas_call(lambda *refs: gram_kernel(freqs, blocks, comps, scaling, *...  12.8 us
    pallas_call x1, Pallas kernels, per_device(): pl.pallas_call(lambda *refs: finish_kernel(freqs, blocks, comps, rank, *r...  12 us
    all_to_all x1, waiting for transfers between devices, per_device(): lax.all_to_all(spread, 'pts', 0, 0, tiled=True)  4.96 us
    all_to_all x1, starting transfers between devices, per_device(): lax.all_to_all(spread, 'pts', 0, 0, tiled=True)  3.89 us
    ppermute x1, starting transfers between devices, per_device(): lax.ppermute(trace, 'freq', [(i, i ^ 2) for i in range(freq_groups)])  2.92 us
    ppermute x1, starting transfers between devices, per_device(): lax.ppermute(trace, 'freq', [(i, i ^ 1) for i in range(freq_groups)])  1.38 us
    ppermute x1, waiting for transfers between devices, per_device(): lax.ppermute(trace, 'freq', [(i, i ^ 1) for i in range(freq_groups)])  1.37 us
  transfers between devices with their start and end apart: 3, of which 2 were waited for; matrix products, arithmetic and copies ran while one was open for 0% of the time, Pallas kernels for 20%

commit v1 on v0

v1 whole, which is shorter than its diff:
```python
import jax
import jax.numpy as jnp
from jax import lax
from jax.experimental import pallas as pl
from jax.experimental.pallas import tpu as pltpu
from jax.sharding import PartitionSpec as P

ITERS = 4
F32 = jnp.float32
BF16 = jnp.bfloat16


def split(x):
    high = x.astype(BF16)
    low = (x - high.astype(F32)).astype(BF16)
    return high, low


def dot_plain(left, right):
    return lax.dot_general(left, right, (((1,), (0,)), ((), ())), preferred_element_type=F32)


def gram_kernel(freqs, blocks, comps, scaling, data, weight, out, buf, lines, sums, sems):
    def read(f):
        return pltpu.make_async_copy(data.at[:, f], buf.at[f], sems.at[f])

    weight_read = pltpu.make_async_copy(weight, lines, sems.at[freqs])
    weight_read.start()
    for f in range(freqs):
        read(f).start()
    weight_read.wait()
    root = jnp.sqrt(lines[...])
    row = lax.broadcasted_iota(jnp.int32, (blocks, blocks), 0)
    col = lax.broadcasted_iota(jnp.int32, (blocks, blocks), 1)
    both = 2 * blocks

    def multiply(pair):
        for half in range(2):
            read(2 * pair + half).wait()
        for half in range(2):
            f = 2 * pair + half
            acc = jnp.zeros((both, 2 * both), F32)
            for c in range(comps):
                x = buf[f, :, c].reshape(both, -1) * root
                high, low = split(x)
                acc = acc + dot_plain(high, jnp.concatenate([high.T, low.T], axis=1))
            sums[f] = acc

    def pack(pair, trace):
        packed = []
        for half in range(2):
            acc = sums[2 * pair + half]
            cross = acc[:, both:]
            full = (acc[:, :both] + (cross + cross.T)) * scaling
            real = full[:blocks, :blocks] + full[blocks:, blocks:]
            imag = full[:blocks, blocks:] - full[blocks:, :blocks]
            packed.append(jnp.where(row <= col, real, imag))
            trace = trace + jnp.where(row == col, real, 0.0)
        wide = jnp.concatenate(packed, axis=1)
        for b in range(blocks // 8):
            start = (pair * (blocks // 8) + b) * 9
            out[pl.ds(start, 8), 0, :] = wide[8 * b : 8 * b + 8, :]
        return trace

    def pair_step(pair, trace):
        trace = pack(pair - 1, trace)
        multiply(pair)
        return trace

    pairs = freqs // 2
    multiply(0)
    trace = lax.fori_loop(1, pairs, pair_step, jnp.zeros((blocks, blocks), F32))
    trace = pack(pairs - 1, trace)
    value = jnp.sum(jnp.sum(trace, axis=1, keepdims=True), axis=0, keepdims=True)
    line = jnp.broadcast_to(value, (1, both))
    for piece in range(freqs // 2 * blocks // 8):
        out[piece * 9 + 8, 0:1, :] = line


def sum_kernel(pieces, arrived, out, trace):
    total = arrived[0:8, 0, :]
    line = arrived[8, 0:1, :]
    for p in range(1, pieces):
        total = total + arrived[9 * p : 9 * p + 8, 0, :]
        line = line + arrived[9 * p + 8, 0:1, :]
    for p in range(pieces):
        out[p] = total
    trace[...] = line


def finish_kernel(freqs, blocks, comps, rank, gram, basis, data, vec_out, ray_out, modes, buf, res, vecs, mats, coefs, sems, out_sems):
    def read(f):
        return pltpu.make_async_copy(data.at[:, f], buf.at[f], sems.at[f])

    def write(f):
        return pltpu.make_async_copy(res.at[:, f], modes.at[:, f], out_sems.at[f])

    for f in range(freqs):
        read(f).start()
    both = 2 * blocks
    row = lax.broadcasted_iota(jnp.int32, (blocks, blocks), 0)
    col = lax.broadcasted_iota(jnp.int32, (blocks, blocks), 1)
    for f in range(freqs):
        packed = gram[f // 2][:, (f % 2) * blocks : (f % 2 + 1) * blocks]
        flipped = packed.T
        real = jnp.where(row <= col, packed, flipped)
        imag = jnp.where(row > col, packed, jnp.where(row < col, -flipped, 0.0))
        top = jnp.concatenate([real, -imag], axis=1)
        bottom = jnp.concatenate([imag, real], axis=1)
        high, low = split(jnp.concatenate([top, bottom], axis=0))
        mats[f] = jnp.concatenate([high, low], axis=1)

    def apply(vec):
        parts = []
        for f in range(freqs):
            high, low = split(vec[f])
            out = dot_plain(jnp.concatenate([high, low], axis=0), mats[f])
            out = out[:rank] + out[rank:]
            parts.append((out[:, both:] + out[:, :both])[None])
        return jnp.concatenate(parts, axis=0)

    lane = lax.broadcasted_iota(jnp.int32, (1, 1, both), 2)
    sub = lax.broadcasted_iota(jnp.int32, (1, rank, 1), 1)
    sign = jnp.where(lane < blocks, -1.0, 1.0).astype(F32)

    def orthonormalize(z):
        turned = pltpu.roll(z.reshape(freqs * rank, both), blocks, 1).reshape(z.shape) * sign
        for k in range(rank):
            base = z[:, k : k + 1, :]
            across = turned[:, k : k + 1, :]
            dot_real = jnp.sum(base * z, axis=2, keepdims=True)
            norm = dot_real[:, k : k + 1, :] * (1.0 / blocks) + 1e-6
            factor = lax.rsqrt(norm)
            if k + 1 < rank:
                dot_imag = jnp.sum(across * z, axis=2, keepdims=True)
                square = factor * factor * (1.0 / blocks)
                low = jnp.where(sub > k, square, 0.0)
                keep = jnp.where(sub == k, factor, 1.0)
                coef_real = dot_real * low
                coef_imag = dot_imag * low
                z, turned = (
                    z * keep - coef_real * base - coef_imag * across,
                    turned * keep - coef_real * across + coef_imag * base,
                )
            else:
                z = jnp.where(sub == k, z * factor, z)
        return z

    vec = jnp.concatenate([basis[0], basis[1]], axis=2)
    vec = lax.fori_loop(0, ITERS, lambda step, v: orthonormalize(apply(v)), vec)
    z = apply(vec)
    ray = jnp.sum(vec * z, axis=2, keepdims=True) * (1.0 / blocks)
    ray_out[...] = jnp.sum(jnp.where(sub == lane, ray, 0.0), axis=1)[:, :rank]
    vecs[0] = vec[:, :, :blocks]
    vecs[1] = vec[:, :, blocks:]
    vec_write = pltpu.make_async_copy(vecs, vec_out, out_sems.at[freqs])
    vec_write.start()
    for f in range(freqs):
        v = vec[f] * (1.0 / blocks)
        real_row = jnp.where(lane[0] < blocks, v, -v)
        imag_row = pltpu.roll(v, blocks, 1)
        high, low = split(jnp.concatenate([real_row, imag_row], axis=0))
        coefs[f] = jnp.concatenate(
            [jnp.concatenate([high, high], axis=1), jnp.concatenate([low, jnp.zeros_like(low)], axis=1)], axis=0
        )

    def project(f, carry):
        read(f).wait()
        coef = coefs[f]
        for c in range(comps):
            x = buf[f, :, c].reshape(both, -1)
            x_high, x_low = split(x)
            out = dot_plain(coef, jnp.concatenate([x_high, x_low], axis=0))
            out = out[: 2 * rank] + out[2 * rank :]
            res[0, f, c] = out[:rank]
            res[1, f, c] = out[rank:]
        write(f).start()
        return carry

    lax.fori_loop(0, freqs, project, 0)
    for f in range(freqs):
        write(f).wait()
    vec_write.wait()


def program(data, quad_weight, basis):
    _, freqs, blocks, comps, points = data.shape
    rank = basis.shape[-1]
    freq_groups = lax.axis_size("freq")
    size = lax.axis_size("pts")
    freq_count = freqs * freq_groups
    scaling = 1.0 / (comps * points * size)
    pieces = freqs // 2 * blocks // 8
    samples = jnp.transpose(data, (0, 1, 3, 2, 4))
    start = jnp.transpose(basis, (0, 1, 3, 2))
    vmem = pl.BlockSpec(memory_space=pltpu.VMEM)
    hbm = pl.BlockSpec(memory_space=pltpu.MemorySpace.HBM)
    packed = pl.pallas_call(
        lambda *refs: gram_kernel(freqs, blocks, comps, scaling, *refs),
        out_shape=pltpu.VMEM((pieces * 9, 1, 2 * blocks), F32),
        in_specs=[hbm, hbm],
        out_specs=vmem,
        scratch_shapes=[
            pltpu.VMEM((freqs, 2, comps, blocks, points), F32),
            pltpu.VMEM((1, points), F32),
            pltpu.VMEM((freqs, 2 * blocks, 4 * blocks), F32),
            pltpu.SemaphoreType.DMA((freqs + 1,)),
        ],
        compiler_params=pltpu.CompilerParams(vmem_limit_bytes=60 * 2**20),
        name="gram",
    )(samples, quad_weight.reshape(1, points))
    arrived = lax.all_to_all(packed, "pts", 0, 0, tiled=True)
    spread, trace = pl.pallas_call(
        lambda *refs: sum_kernel(size, *refs),
        out_shape=(
            jax.ShapeDtypeStruct((size, 8, 2 * blocks), F32),
            jax.ShapeDtypeStruct((1, 2 * blocks), F32),
        ),
        in_specs=[vmem],
        out_specs=(vmem, vmem),
        compiler_params=pltpu.CompilerParams(vmem_limit_bytes=2 * 2**20),
        name="total",
    )(arrived)
    trace = trace + lax.ppermute(trace, "freq", [(i, i ^ 1) for i in range(freq_groups)])
    gram = lax.all_to_all(spread, "pts", 0, 0, tiled=True).reshape(freqs // 2, blocks, 2 * blocks)
    other = lax.ppermute(trace, "freq", [(i, freq_groups - 1 - i) for i in range(freq_groups)])
    vec, ray, modes = pl.pallas_call(
        lambda *refs: finish_kernel(freqs, blocks, comps, rank, *refs),
        out_shape=(
            jax.ShapeDtypeStruct((2, freqs, rank, blocks), F32),
            pltpu.VMEM((freqs, rank), F32),
            jax.ShapeDtypeStruct((2, freqs, comps, rank, points), F32),
        ),
        in_specs=[vmem, vmem, hbm],
        out_specs=(hbm, vmem, hbm),
        scratch_shapes=[
            pltpu.VMEM((freqs, 2, comps, blocks, points), F32),
            pltpu.VMEM((2, freqs, comps, rank, points), F32),
            pltpu.VMEM((2, freqs, rank, blocks), F32),
            pltpu.VMEM((freqs, 2 * blocks, 4 * blocks), BF16),
            pltpu.VMEM((freqs, 4 * rank, 4 * blocks), BF16),
            pltpu.SemaphoreType.DMA((freqs,)),
            pltpu.SemaphoreType.DMA((freqs + 1,)),
        ],
        compiler_params=pltpu.CompilerParams(vmem_limit_bytes=52 * 2**20),
        name="finish",
    )(gram, start, samples)
    total = (trace + other)[0, 0]
    spectrum = ray * (freq_count * blocks) / total
    return (
        jnp.transpose(vec, (0, 1, 3, 2)),
        spectrum,
        jnp.transpose(modes, (0, 1, 3, 2, 4)),
    )


def solution(mesh):
    in_specs = (P(None, "freq", None, None, "pts"), P("pts"), P(None, "freq", None, None))
    out_specs = (P(None, "freq", None, None), P("freq", None), P(None, "freq", None, None, "pts"))
    return jax.shard_map(
        program, mesh=mesh, in_specs=in_specs, out_specs=out_specs, check_vma=False
    )
```

time: 59.5 us -> 47.5 us (0.80)
  Pallas kernels: 25.5 us -> 17.4 us
  waiting for transfers between devices: 6.33 us -> 3.59 us
  other arithmetic: 1.33 us -> 0.64 us
    pallas_call x3, Pallas kernels: 25.5 us -> 17.4 us  [the longest x1 8.9 us: program(): pl.pallas_call(lambda *refs: finish_kernel(freqs, blocks, comps, rank, *r...]
    all_to_all x1, waiting for transfers between devices: 4.96 us -> 0.97 us  [program(): lax.all_to_all(spread, 'pts', 0, 0, tiled=True)]
    ppermute x2, waiting for transfers between devices: 1.37 us -> 2.62 us  [the longest x1 1.37 us: program(): lax.ppermute(trace, 'freq', [(i, i ^ 1) for i in range(freq_groups)])]
    div x1, other arithmetic: 1.32 us -> 0.63 us  [program(): spectrum = ray * (freq_count * blocks) / total]
  transfers between devices with their start and end apart: 3 -> 3, of which waited for: 2 -> 3; matrix products, arithmetic and copies ran while one was open for 0% -> 0% of each run, Pallas kernels for 20% -> 0%
where the time goes in v1:
time: 47.5 us; the launch traced here: 47.3 us
  Pallas kernels  17.4 us (37%)
  blocking collectives  17 us (36%)
  starting transfers between devices  8.01 us (17%)
  waiting for transfers between devices  3.59 us (8%)
  between operations  0.67 us (1%)
  other arithmetic  0.64 us (1%)
    all_to_all x1, blocking collectives, program(): arrived = lax.all_to_all(packed, 'pts', 0, 0, tiled=True)  17 us
    pallas_call x1, Pallas kernels, program(): pl.pallas_call(lambda *refs: finish_kernel(freqs, blocks, comps, rank, *r...  8.9 us
    pallas_call x1, Pallas kernels, program(): pl.pallas_call(lambda *refs: gram_kernel(freqs, blocks, comps, scaling, *...  7.77 us
    all_to_all x1, starting transfers between devices, program(): lax.all_to_all(spread, 'pts', 0, 0, tiled=True)  3.9 us
    ppermute x1, starting transfers between devices, program(): lax.ppermute(trace, 'freq', [(i, freq_groups - 1 - i) for i in range(freq...  2.74 us
    ppermute x1, starting transfers between devices, program(): lax.ppermute(trace, 'freq', [(i, i ^ 1) for i in range(freq_groups)])  1.38 us
    ppermute x1, waiting for transfers between devices, program(): lax.ppermute(trace, 'freq', [(i, i ^ 1) for i in range(freq_groups)])  1.37 us
    ppermute x1, waiting for transfers between devices, program(): lax.ppermute(trace, 'freq', [(i, freq_groups - 1 - i) for i in range(freq...  1.25 us
  transfers between devices with their start and end apart: 3, of which 3 were waited for; matrix products, arithmetic and copies ran while one was open for 0% of the time, Pallas kernels for 0%

profile of v1, /device:TPU:1, one launch (start us, length us, event | category | flops | bytes accessed | tf_op | source)
XLA Modules:
  0.0 47.3 jit_solution(14928652834696977390)
XLA Ops:
  0.6 0.0 copy-start
  0.6 7.8 %gram.1 = f32[288,1,128]{2,1,0:T(1,128)S(1)} custom-call(f32[2,8,3,64,1024]{4,3,2,1,0:T(8,128)} %bitcast.10, f32[1,1024]{1,0:T(1,128)} %bitcast.12), custom_call_target="tpu_custom_call" | custom-call | tf_op jit(solution)/shard_map/gram/pallas_call | solution.py:198
  8.4 17.0 %all_to_all.10.refs_0_ = f32[288,1,128]{2,1,0:T(1,128)S(1)} all-to-all(f32[288,1,128]{2,1,0:T(1,128)S(1)} %gram.1), channel_id=1, replica_groups=mesh['freq'=4,'pts'=32] {'pts'}, dimensions={0} | all-to-all | bytes 294912 | tf_op jit(solution)/shard_map/all_to_all | solution.py:212
  25.4 0.7 %total.1 = (f32[32,8,128]{2,1,0:T(8,128)}, f32[1,128]{1,0:T(1,128)S(1)}) custom-call(f32[288,1,128]{2,1,0:T(1,128)S(1)} %all_to_all.10.refs_0_), custom_call_target="tpu_custom_call" | custom-call | tf_op jit(solution)/shard_map/total/pallas_call | solution.py:213
  26.1 3.9 %all-to-all-start.1 = ((f32[32,8,128]{2,1,0:T(8,128)}), f32[32,8,128]{2,1,0:T(8,128)S(1)}, u32[]{:S(2)}, u32[]{:S(2)}) async-start(f32[32,8,128]{2,1,0:T(8,128)} %get-tuple-element.8), calls=%async_computation.1 | async-start | bytes 262144 | tf_op jit(solution)/shard_map/all_to_all | solution.py:225
  30.0 1.4 %collective-permute-start = (f32[1,128]{1,0:T(1,128)S(1)}, f32[1,128]{1,0:T(1,128)S(1)}, u32[]{:S(2)}, u32[]{:S(2)}) collective-permute-start(f32[1,128]{1,0:T(1,128)S(1)} %get-tuple-element.11), channel_id=1, source_target_pairs={{0,32},{32,0},{64,96},{96,64},{1,33},{33,1},{65,97},{97,65},{2,34}... | collective-permute-start | bytes 1544 | tf_op jit(solution)/shard_map/ppermute | solution.py:224
  31.4 1.4 %collective-permute-done = f32[1,128]{1,0:T(1,128)S(1)} collective-permute-done((f32[1,128]{1,0:T(1,128)S(1)}, f32[1,128]{1,0:T(1,128)S(1)}, u32[]{:S(2)}, u32[]{:S(2)}) %collective-permute-start) | collective-permute-done | bytes 544 | tf_op jit(solution)/shard_map/ppermute | solution.py:224
  32.8 2.7 %collective-permute-start.1 = (f32[1,128]{1,0:T(1,128)S(1)}, f32[1,128]{1,0:T(1,128)S(1)}, u32[]{:S(2)}, u32[]{:S(2)}) collective-permute-start(f32[1,128]{1,0:T(1,128)S(1)} %add.6), channel_id=1, source_target_pairs={{0,96},{32,64},{64,32},{96,0},{1,97},{33,65},{65,33},{97,1},{2,98}... | collective-permute-start | bytes 1544 | tf_op jit(solution)/shard_map/ppermute | solution.py:226
  35.5 1.3 %collective-permute-done.1 = f32[1,128]{1,0:T(1,128)S(1)} collective-permute-done((f32[1,128]{1,0:T(1,128)S(1)}, f32[1,128]{1,0:T(1,128)S(1)}, u32[]{:S(2)}, u32[]{:S(2)}) %collective-permute-start.1) | collective-permute-done | bytes 544 | tf_op jit(solution)/shard_map/ppermute | solution.py:226
  36.8 1.0 %all-to-all-done.1 = f32[32,8,128]{2,1,0:T(8,128)S(1)} async-done(((f32[32,8,128]{2,1,0:T(8,128)}), f32[32,8,128]{2,1,0:T(8,128)S(1)}, u32[]{:S(2)}, u32[]{:S(2)}) %all-to-all-start.1) | async-done | bytes 131104 | tf_op jit(solution)/shard_map/all_to_all | solution.py:225
  37.7 0.0 copy-done
  37.7 8.9 %finish.1 = (f32[2,8,8,64]{3,2,1,0:T(8,128)}, f32[8,8]{1,0:T(8,128)S(1)}, f32[2,8,3,8,1024]{4,3,2,1,0:T(8,128)}) custom-call(f32[4,64,128]{2,1,0:T(8,128)S(1)} %bitcast.8, f32[2,8,8,64]{3,2,1,0:T(8,128)S(1)} %bitcast.9, f32[2,8,3,64,1024]{4,3,2,1,0:T(8,128)} %bitcast.11), custom_call_target="tpu_custom_call" | custom-call | tf_op jit(solution)/shard_map/finish/pallas_call | solution.py:227
  46.6 0.6 %multiply_divide_fusion = f32[8,8]{1,0:T(8,128)} fusion(f32[8,8]{1,0:T(8,128)S(1)} %get-tuple-element.10, f32[]{:T(128)S(1)} %bitcast.13), kind=kLoop, calls=%fused_computation | loop fusion | flops 128 | bytes 516 | tf_op jit(solution)/shard_map/div | solution.py:249
  (2 shorter events, 0.0 us)
Async XLA Ops:
  0.6 37.1 %copy-start = (f32[2,8,64,8]{2,3,1,0:T(8,128)S(1)}, f32[2,8,64,8]{2,3,1,0:T(8,128)}, u32[]{:S(2)}) copy-start(f32[2,8,64,8]{2,3,1,0:T(8,128)} %param.5) | copy-start | bytes 98308
  26.1 11.6 %all-to-all-start.1 = ((f32[32,8,128]{2,1,0:T(8,128)}), f32[32,8,128]{2,1,0:T(8,128)S(1)}, u32[]{:S(2)}, u32[]{:S(2)}) async-start(f32[32,8,128]{2,1,0:T(8,128)} %get-tuple-element.8), calls=%async_computation.1 | async-start | bytes 262144 | tf_op jit(solution)/shard_map/all_to_all | solution.py:225
  30.0 2.7 %collective-permute-start = (f32[1,128]{1,0:T(1,128)S(1)}, f32[1,128]{1,0:T(1,128)S(1)}, u32[]{:S(2)}, u32[]{:S(2)}) collective-permute-start(f32[1,128]{1,0:T(1,128)S(1)} %get-tuple-element.11), channel_id=1, source_target_pairs={{0,32},{32,0},{64,96},{96,64},{1,33},{33,1},{65,97},{97,65},{2,34}... | collective-permute-start | bytes 1544 | tf_op jit(solution)/shard_map/ppermute | solution.py:224
  32.8 4.0 %collective-permute-start.1 = (f32[1,128]{1,0:T(1,128)S(1)}, f32[1,128]{1,0:T(1,128)S(1)}, u32[]{:S(2)}, u32[]{:S(2)}) collective-permute-start(f32[1,128]{1,0:T(1,128)S(1)} %add.6), channel_id=1, source_target_pairs={{0,96},{32,64},{64,32},{96,0},{1,97},{33,65},{65,33},{97,1},{2,98}... | collective-permute-start | bytes 1544 | tf_op jit(solution)/shard_map/ppermute | solution.py:226

commit v2 on v1

--- a/solution.py
+++ b/solution.py
@@ -6,6 +6,7 @@
 from jax.sharding import PartitionSpec as P
 
 ITERS = 4
+TOGETHER = 4
 F32 = jnp.float32
 BF16 = jnp.bfloat16
 
@@ -14,6 +15,10 @@
     high = x.astype(BF16)
     low = (x - high.astype(F32)).astype(BF16)
     return high, low
+
+
+def dot_rows(left, right):
+    return lax.dot_general(left, right, (((1,), (1,)), ((), ())), preferred_element_type=F32)
 
 
 def dot_plain(left, right):
@@ -34,11 +39,11 @@
     col = lax.broadcasted_iota(jnp.int32, (blocks, blocks), 1)
     both = 2 * blocks
 
-    def multiply(pair):
-        for half in range(2):
-            read(2 * pair + half).wait()
-        for half in range(2):
-            f = 2 * pair + half
+    def multiply(first, count):
+        for f in range(count):
+            read(first + f).wait()
+        for f in range(count):
+            f = first + f
             acc = jnp.zeros((both, 2 * both), F32)
             for c in range(comps):
                 x = buf[f, :, c].reshape(both, -1) * root
@@ -64,12 +69,15 @@
 
     def pair_step(pair, trace):
         trace = pack(pair - 1, trace)
-        multiply(pair)
+        multiply(2 * pair, 2)
         return trace
 
     pairs = freqs // 2
-    multiply(0)
-    trace = lax.fori_loop(1, pairs, pair_step, jnp.zeros((blocks, blocks), F32))
+    multiply(0, 1)
+    multiply(1, 1)
+    trace = jnp.zeros((blocks, blocks), F32)
+    for pair in range(1, pairs):
+        trace = pair_step(pair, trace)
     trace = pack(pairs - 1, trace)
     value = jnp.sum(jnp.sum(trace, axis=1, keepdims=True), axis=0, keepdims=True)
     line = jnp.broadcast_to(value, (1, both))
@@ -88,7 +96,10 @@
     trace[...] = line
 
 
-def finish_kernel(freqs, blocks, comps, rank, gram, basis, data, vec_out, ray_out, modes, buf, res, vecs, mats, coefs, sems, out_sems):
+def finish_kernel(freqs, blocks, comps, rank, groups, gram, basis, data, *refs):
+    traces = refs[:groups]
+    vec_out, spectrum, modes, buf, res, vecs, rates, mats, coefs, sems, out_sems = refs[groups:]
+
     def read(f):
         return pltpu.make_async_copy(data.at[:, f], buf.at[f], sems.at[f])
 
@@ -147,10 +158,17 @@
         return z
 
     vec = jnp.concatenate([basis[0], basis[1]], axis=2)
-    vec = lax.fori_loop(0, ITERS, lambda step, v: orthonormalize(apply(v)), vec)
+    for step in range(ITERS):
+        vec = orthonormalize(apply(vec))
     z = apply(vec)
     ray = jnp.sum(vec * z, axis=2, keepdims=True) * (1.0 / blocks)
-    ray_out[...] = jnp.sum(jnp.where(sub == lane, ray, 0.0), axis=1)[:, :rank]
+    total = traces[0][...]
+    for line in traces[1:]:
+        total = total + line[...]
+    energy = jnp.sum(jnp.where(sub == lane, ray, 0.0), axis=1) * (freqs * groups * blocks)
+    rates[...] = (energy / total)[:, :rank]
+    rate_write = pltpu.make_async_copy(rates, spectrum, out_sems.at[freqs + 1])
+    rate_write.start()
     vecs[0] = vec[:, :, :blocks]
     vecs[1] = vec[:, :, blocks:]
     vec_write = pltpu.make_async_copy(vecs, vec_out, out_sems.at[freqs])
@@ -164,26 +182,31 @@
             [jnp.concatenate([high, high], axis=1), jnp.concatenate([low, jnp.zeros_like(low)], axis=1)], axis=0
         )
 
-    def project(f, carry):
-        read(f).wait()
-        coef = coefs[f]
-        for c in range(comps):
-            x = buf[f, :, c].reshape(both, -1)
-            x_high, x_low = split(x)
-            out = dot_plain(coef, jnp.concatenate([x_high, x_low], axis=0))
-            out = out[: 2 * rank] + out[2 * rank :]
-            res[0, f, c] = out[:rank]
-            res[1, f, c] = out[rank:]
-        write(f).start()
+    def project(step, carry):
+        first = step * TOGETHER
+        for f in range(TOGETHER):
+            read(first + f).wait()
+        for f in range(TOGETHER):
+            f = first + f
+            coef = coefs[f]
+            for c in range(comps):
+                x = buf[f, :, c].reshape(both, -1)
+                x_high, x_low = split(x)
+                out = dot_plain(coef, jnp.concatenate([x_high, x_low], axis=0))
+                out = out[: 2 * rank] + out[2 * rank :]
+                res[0, f, c] = out[:rank]
+                res[1, f, c] = out[rank:]
+            write(f).start()
         return carry
 
-    lax.fori_loop(0, freqs, project, 0)
+    lax.fori_loop(0, freqs // TOGETHER, project, 0)
     for f in range(freqs):
         write(f).wait()
     vec_write.wait()
-
-
-def program(data, quad_weight, basis):
+    rate_write.wait()
+
+
+def per_device(data, quad_weight, basis):
     _, freqs, blocks, comps, points = data.shape
     rank = basis.shape[-1]
     freq_groups = lax.axis_size("freq")
@@ -221,32 +244,34 @@
         compiler_params=pltpu.CompilerParams(vmem_limit_bytes=2 * 2**20),
         name="total",
     )(arrived)
-    trace = trace + lax.ppermute(trace, "freq", [(i, i ^ 1) for i in range(freq_groups)])
+    others = [
+        lax.ppermute(trace, "freq", [(i, (i + d) % freq_groups) for i in range(freq_groups)])
+        for d in range(1, freq_groups)
+    ]
     gram = lax.all_to_all(spread, "pts", 0, 0, tiled=True).reshape(freqs // 2, blocks, 2 * blocks)
-    other = lax.ppermute(trace, "freq", [(i, freq_groups - 1 - i) for i in range(freq_groups)])
-    vec, ray, modes = pl.pallas_call(
-        lambda *refs: finish_kernel(freqs, blocks, comps, rank, *refs),
+    traces = [trace, *others]
+    vec, spectrum, modes = pl.pallas_call(
+        lambda *refs: finish_kernel(freqs, blocks, comps, rank, freq_groups, *refs),
         out_shape=(
             jax.ShapeDtypeStruct((2, freqs, rank, blocks), F32),
-            pltpu.VMEM((freqs, rank), F32),
+            jax.ShapeDtypeStruct((freqs, rank), F32),
             jax.ShapeDtypeStruct((2, freqs, comps, rank, points), F32),
         ),
-        in_specs=[vmem, vmem, hbm],
-        out_specs=(hbm, vmem, hbm),
+        in_specs=[vmem, vmem, hbm] + [vmem] * freq_groups,
+        out_specs=(hbm, hbm, hbm),
         scratch_shapes=[
             pltpu.VMEM((freqs, 2, comps, blocks, points), F32),
             pltpu.VMEM((2, freqs, comps, rank, points), F32),
             pltpu.VMEM((2, freqs, rank, blocks), F32),
+            pltpu.VMEM((freqs, rank), F32),
             pltpu.VMEM((freqs, 2 * blocks, 4 * blocks), BF16),
             pltpu.VMEM((freqs, 4 * rank, 4 * blocks), BF16),
             pltpu.SemaphoreType.DMA((freqs,)),
-            pltpu.SemaphoreType.DMA((freqs + 1,)),
+            pltpu.SemaphoreType.DMA((freqs + 2,)),
         ],
         compiler_params=pltpu.CompilerParams(vmem_limit_bytes=52 * 2**20),
         name="finish",
-    )(gram, start, samples)
-    total = (trace + other)[0, 0]
-    spectrum = ray * (freq_count * blocks) / total
+    )(gram, start, samples, *traces)
     return (
         jnp.transpose(vec, (0, 1, 3, 2)),
         spectrum,
@@ -258,5 +283,5 @@
     in_specs = (P(None, "freq", None, None, "pts"), P("pts"), P(None, "freq", None, None))
     out_specs = (P(None, "freq", None, None), P("freq", None), P(None, "freq", None, None, "pts"))
     return jax.shard_map(
-        program, mesh=mesh, in_specs=in_specs, out_specs=out_specs, check_vma=False
+        per_device, mesh=mesh, in_specs=in_specs, out_specs=out_specs, check_vma=False
     )

time: 47.5 us -> 44.9 us (0.945)
  Pallas kernels: 17.4 us -> 15.5 us
  other arithmetic: 0.64 us -> 0 us
    pallas_call x3, Pallas kernels: 17.4 us -> 15.5 us  [the longest x1 7.55 us: per_device(): pl.pallas_call(lambda *refs: finish_kernel(freqs, blocks, comps, rank, fr...]
    div x1 -> x0, other arithmetic: 0.63 us -> none  [program(): spectrum = ray * (freq_count * blocks) / total]
    ppermute x2 -> x3, waiting for transfers between devices: 2.62 us -> 3.23 us  [per_device(): lax.ppermute(trace, 'freq', [(i, (i + d) % freq_groups) for i in range(fr...]
    ppermute x2 -> x3, starting transfers between devices: 4.11 us -> 3.85 us  [per_device(): lax.ppermute(trace, 'freq', [(i, (i + d) % freq_groups) for i in range(fr...]
  transfers between devices with their start and end apart: 3 -> 4, of which waited for: 3 -> 3; matrix products, arithmetic and copies ran while one was open for 0% -> 0% of each run, Pallas kernels for 0% -> 0%
where the time goes in v2:
time: 44.9 us; the launch traced here: 44.7 us
  blocking collectives  17 us (38%)
  Pallas kernels  15.5 us (35%)
  starting transfers between devices  7.74 us (17%)
  waiting for transfers between devices  3.86 us (9%)
  between operations  0.66 us (1%)
    all_to_all x1, blocking collectives, per_device(): arrived = lax.all_to_all(packed, 'pts', 0, 0, tiled=True)  17 us
    pallas_call x1, Pallas kernels, per_device(): pl.pallas_call(lambda *refs: finish_kernel(freqs, blocks, comps, rank, fr...  7.55 us
    pallas_call x1, Pallas kernels, per_device(): pl.pallas_call(lambda *refs: gram_kernel(freqs, blocks, comps, scaling, *...  7.19 us
    all_to_all x1, starting transfers between devices, per_device(): lax.all_to_all(spread, 'pts', 0, 0, tiled=True)  3.9 us
    ppermute x3, starting transfers between devices, per_device(): lax.ppermute(trace, 'freq', [(i, (i + d) % freq_groups) for i in range(fr...  3.85 us
    ppermute x3, waiting for transfers between devices, per_device(): lax.ppermute(trace, 'freq', [(i, (i + d) % freq_groups) for i in range(fr...  3.23 us
  transfers between devices with their start and end apart: 4, of which 3 were waited for; matrix products, arithmetic and copies ran while one was open for 0% of the time, Pallas kernels for 0%

profile of v2, /device:TPU:1, one launch (start us, length us, event | category | flops | bytes accessed | tf_op | source)
XLA Modules:
  0.0 44.7 jit_solution(16550957898622149378)
XLA Ops:
  0.6 0.0 copy-start
  0.6 7.2 %gram.1 = f32[288,1,128]{2,1,0:T(1,128)S(1)} custom-call(f32[2,8,3,64,1024]{4,3,2,1,0:T(8,128)} %bitcast.8, f32[1,1024]{1,0:T(1,128)} %bitcast.10), custom_call_target="tpu_custom_call" | custom-call | tf_op jit(solution)/shard_map/gram/pallas_call | solution.py:221
  7.8 17.0 %all_to_all.10.refs_0_ = f32[288,1,128]{2,1,0:T(1,128)S(1)} all-to-all(f32[288,1,128]{2,1,0:T(1,128)S(1)} %gram.1), channel_id=1, replica_groups=mesh['freq'=4,'pts'=32] {'pts'}, dimensions={0} | all-to-all | bytes 294912 | tf_op jit(solution)/shard_map/all_to_all | solution.py:235
  24.8 0.7 %total.1 = (f32[32,8,128]{2,1,0:T(8,128)}, f32[1,128]{1,0:T(1,128)S(1)}) custom-call(f32[288,1,128]{2,1,0:T(1,128)S(1)} %all_to_all.10.refs_0_), custom_call_target="tpu_custom_call" | custom-call | tf_op jit(solution)/shard_map/total/pallas_call | solution.py:236
  25.5 3.9 %all-to-all-start.1 = ((f32[32,8,128]{2,1,0:T(8,128)}), f32[32,8,128]{2,1,0:T(8,128)S(1)}, u32[]{:S(2)}, u32[]{:S(2)}) async-start(f32[32,8,128]{2,1,0:T(8,128)} %get-tuple-element.8), calls=%async_computation.1 | async-start | bytes 262144 | tf_op jit(solution)/shard_map/all_to_all | solution.py:251
  29.4 2.8 %collective-permute-start.2 = (f32[1,128]{1,0:T(1,128)S(1)}, f32[1,128]{1,0:T(1,128)S(1)}, u32[]{:S(2)}, u32[]{:S(2)}) collective-permute-start(f32[1,128]{1,0:T(1,128)S(1)} %get-tuple-element.9.refs_3_), channel_id=1, source_target_pairs={{0,96},{32,0},{64,32},{96,64},{1,97},{33,1},{65,33},{97,65},{2,98}... | collective-permute-start | bytes 1544 | tf_op jit(solution)/shard_map/ppermute | solution.py:248
  32.2 0.3 collective-permute-start.1
  32.6 0.7 %collective-permute-start = (f32[1,128]{1,0:T(1,128)S(1)}, f32[1,128]{1,0:T(1,128)S(1)}, u32[]{:S(2)}, u32[]{:S(2)}) collective-permute-start(f32[1,128]{1,0:T(1,128)S(1)} %get-tuple-element.9.refs_3_), channel_id=1, source_target_pairs={{0,32},{32,64},{64,96},{96,0},{1,33},{33,65},{65,97},{97,1},{2,34}... | collective-permute-start | bytes 1544 | tf_op jit(solution)/shard_map/ppermute | solution.py:248
  33.3 0.0 collective-permute-done.2.refs_6_
  33.3 3.2 %collective-permute-done.1.refs_5_ = f32[1,128]{1,0:T(1,128)S(1)} collective-permute-done((f32[1,128]{1,0:T(1,128)S(1)}, f32[1,128]{1,0:T(1,128)S(1)}, u32[]{:S(2)}, u32[]{:S(2)}) %collective-permute-start.1) | collective-permute-done | bytes 544 | tf_op jit(solution)/shard_map/ppermute | solution.py:248
  36.5 0.1 collective-permute-done.refs_4_
  36.5 0.6 %all-to-all-done.1 = f32[32,8,128]{2,1,0:T(8,128)S(1)} async-done(((f32[32,8,128]{2,1,0:T(8,128)}), f32[32,8,128]{2,1,0:T(8,128)S(1)}, u32[]{:S(2)}, u32[]{:S(2)}) %all-to-all-start.1) | async-done | bytes 131104 | tf_op jit(solution)/shard_map/all_to_all | solution.py:251
  37.1 0.0 copy-done
  37.2 7.5 %finish.1 = (f32[2,8,8,64]{3,2,1,0:T(8,128)}, f32[8,8]{1,0:T(8,128)}, f32[2,8,3,8,1024]{4,3,2,1,0:T(8,128)}) custom-call(f32[4,64,128]{2,1,0:T(8,128)S(1)} %bitcast.6, f32[2,8,8,64]{3,2,1,0:T(8,128)S(1)} %bitcast.7, f32[2,8,3,64,1024]{4,3,2,1,0:T(8,128)} %bitcast.9, f32[1,128]{1,0:T(1,128)S(1)} %get-tuple-element.9.refs_3_, ...), custom_call_target="tpu_custom_call" | custom-call | tf_op jit(solution)/shard_map/finish/pallas_call | solution.py:253
Async XLA Ops:
  0.6 36.5 %copy-start = (f32[2,8,64,8]{2,3,1,0:T(8,128)S(1)}, f32[2,8,64,8]{2,3,1,0:T(8,128)}, u32[]{:S(2)}) copy-start(f32[2,8,64,8]{2,3,1,0:T(8,128)} %param.5) | copy-start | bytes 98308
  25.5 11.6 %all-to-all-start.1 = ((f32[32,8,128]{2,1,0:T(8,128)}), f32[32,8,128]{2,1,0:T(8,128)S(1)}, u32[]{:S(2)}, u32[]{:S(2)}) async-start(f32[32,8,128]{2,1,0:T(8,128)} %get-tuple-element.8), calls=%async_computation.1 | async-start | bytes 262144 | tf_op jit(solution)/shard_map/all_to_all | solution.py:251
  29.4 3.9 %collective-permute-start.2 = (f32[1,128]{1,0:T(1,128)S(1)}, f32[1,128]{1,0:T(1,128)S(1)}, u32[]{:S(2)}, u32[]{:S(2)}) collective-permute-start(f32[1,128]{1,0:T(1,128)S(1)} %get-tuple-element.9.refs_3_), channel_id=1, source_target_pairs={{0,96},{32,0},{64,32},{96,64},{1,97},{33,1},{65,33},{97,65},{2,98}... | collective-permute-start | bytes 1544 | tf_op jit(solution)/shard_map/ppermute | solution.py:248
  32.2 4.2 %collective-permute-start.1 = (f32[1,128]{1,0:T(1,128)S(1)}, f32[1,128]{1,0:T(1,128)S(1)}, u32[]{:S(2)}, u32[]{:S(2)}) collective-permute-start(f32[1,128]{1,0:T(1,128)S(1)} %get-tuple-element.9.refs_3_), channel_id=1, source_target_pairs={{0,64},{32,96},{64,0},{96,32},{1,65},{33,97},{65,1},{97,33},{2,66}... | collective-permute-start | bytes 1544 | tf_op jit(solution)/shard_map/ppermute | solution.py:248
  32.6 3.9 %collective-permute-start = (f32[1,128]{1,0:T(1,128)S(1)}, f32[1,128]{1,0:T(1,128)S(1)}, u32[]{:S(2)}, u32[]{:S(2)}) collective-permute-start(f32[1,128]{1,0:T(1,128)S(1)} %get-tuple-element.9.refs_3_), channel_id=1, source_target_pairs={{0,32},{32,64},{64,96},{96,0},{1,33},{33,65},{65,97},{97,1},{2,34}... | collective-permute-start | bytes 1544 | tf_op jit(solution)/shard_map/ppermute | solution.py:248

commit v3 on v2

--- a/solution.py
+++ b/solution.py
@@ -29,9 +29,14 @@
     def read(f):
         return pltpu.make_async_copy(data.at[:, f], buf.at[f], sems.at[f])
 
+    def read_first(c):
+        return pltpu.make_async_copy(data.at[:, 0, c], buf.at[0, :, c], sems.at[freqs + 1 + c])
+
     weight_read = pltpu.make_async_copy(weight, lines, sems.at[freqs])
     weight_read.start()
-    for f in range(freqs):
+    for c in range(comps):
+        read_first(c).start()
+    for f in range(1, freqs):
         read(f).start()
     weight_read.wait()
     root = jnp.sqrt(lines[...])
@@ -39,16 +44,18 @@
     col = lax.broadcasted_iota(jnp.int32, (blocks, blocks), 1)
     both = 2 * blocks
 
+    def product(f, c):
+        x = buf[f, :, c].reshape(both, -1) * root
+        high, low = split(x)
+        return dot_plain(high, jnp.concatenate([high.T, low.T], axis=1))
+
     def multiply(first, count):
         for f in range(count):
             read(first + f).wait()
-        for f in range(count):
-            f = first + f
+        for f in range(first, first + count):
             acc = jnp.zeros((both, 2 * both), F32)
             for c in range(comps):
-                x = buf[f, :, c].reshape(both, -1) * root
-                high, low = split(x)
-                acc = acc + dot_plain(high, jnp.concatenate([high.T, low.T], axis=1))
+                acc = acc + product(f, c)
             sums[f] = acc
 
     def pack(pair, trace):
@@ -73,7 +80,11 @@
         return trace
 
     pairs = freqs // 2
-    multiply(0, 1)
+    acc = jnp.zeros((both, 2 * both), F32)
+    for c in range(comps):
+        read_first(c).wait()
+        acc = acc + product(0, c)
+    sums[0] = acc
     multiply(1, 1)
     trace = jnp.zeros((blocks, blocks), F32)
     for pair in range(1, pairs):
@@ -139,10 +150,10 @@
         for k in range(rank):
             base = z[:, k : k + 1, :]
             across = turned[:, k : k + 1, :]
-            dot_real = jnp.sum(base * z, axis=2, keepdims=True)
-            norm = dot_real[:, k : k + 1, :] * (1.0 / blocks) + 1e-6
+            norm = jnp.sum(base * base, axis=2, keepdims=True) * (1.0 / blocks) + 1e-6
             factor = lax.rsqrt(norm)
             if k + 1 < rank:
+                dot_real = jnp.sum(base * z, axis=2, keepdims=True)
                 dot_imag = jnp.sum(across * z, axis=2, keepdims=True)
                 square = factor * factor * (1.0 / blocks)
                 low = jnp.where(sub > k, square, 0.0)
@@ -227,7 +238,7 @@
             pltpu.VMEM((freqs, 2, comps, blocks, points), F32),
             pltpu.VMEM((1, points), F32),
             pltpu.VMEM((freqs, 2 * blocks, 4 * blocks), F32),
-            pltpu.SemaphoreType.DMA((freqs + 1,)),
+            pltpu.SemaphoreType.DMA((freqs + 1 + comps,)),
         ],
         compiler_params=pltpu.CompilerParams(vmem_limit_bytes=60 * 2**20),
         name="gram",

time: 44.9 us -> 44.9 us (level)
  transfers between devices with their start and end apart: 4 -> 4, of which waited for: 3 -> 2; matrix products, arithmetic and copies ran while one was open for 0% -> 0% of each run, Pallas kernels for 0% -> 0%
where the time goes in v3:
time: 44.9 us; the launch traced here: 44.7 us
  blocking collectives  17 us (38%)
  Pallas kernels  15.4 us (34%)
  starting transfers between devices  7.75 us (17%)
  waiting for transfers between devices  3.86 us (9%)
  between operations  0.66 us (1%)
    all_to_all x1, blocking collectives, per_device(): arrived = lax.all_to_all(packed, 'pts', 0, 0, tiled=True)  17 us
    pallas_call x1, Pallas kernels, per_device(): pl.pallas_call(lambda *refs: finish_kernel(freqs, blocks, comps, rank, fr...  7.54 us
    pallas_call x1, Pallas kernels, per_device(): pl.pallas_call(lambda *refs: gram_kernel(freqs, blocks, comps, scaling, *...  7.16 us
    all_to_all x1, starting transfers between devices, per_device(): lax.all_to_all(spread, 'pts', 0, 0, tiled=True)  3.9 us
    ppermute x3, starting transfers between devices, per_device(): lax.ppermute(trace, 'freq', [(i, (i + d) % freq_groups) for i in range(fr...  3.85 us
    ppermute x3, waiting for transfers between devices, per_device(): lax.ppermute(trace, 'freq', [(i, (i + d) % freq_groups) for i in range(fr...  3.22 us
  transfers between devices with their start and end apart: 4, of which 2 were waited for; matrix products, arithmetic and copies ran while one was open for 0% of the time, Pallas kernels for 0%

profile of v3, /device:TPU:1, one launch (start us, length us, event | category | flops | bytes accessed | tf_op | source)
XLA Modules:
  0.0 44.7 jit_solution(1372160529318239823)
XLA Ops:
  0.6 0.0 copy-start
  0.6 7.2 %gram.1 = f32[288,1,128]{2,1,0:T(1,128)S(1)} custom-call(f32[2,8,3,64,1024]{4,3,2,1,0:T(8,128)} %bitcast.8, f32[1,1024]{1,0:T(1,128)} %bitcast.10), custom_call_target="tpu_custom_call" | custom-call | tf_op jit(solution)/shard_map/gram/pallas_call | solution.py:232
  7.8 17.0 %all_to_all.10.refs_0_ = f32[288,1,128]{2,1,0:T(1,128)S(1)} all-to-all(f32[288,1,128]{2,1,0:T(1,128)S(1)} %gram.1), channel_id=1, replica_groups=mesh['freq'=4,'pts'=32] {'pts'}, dimensions={0} | all-to-all | bytes 294912 | tf_op jit(solution)/shard_map/all_to_all | solution.py:246
  24.8 0.7 %total.1 = (f32[32,8,128]{2,1,0:T(8,128)}, f32[1,128]{1,0:T(1,128)S(1)}) custom-call(f32[288,1,128]{2,1,0:T(1,128)S(1)} %all_to_all.10.refs_0_), custom_call_target="tpu_custom_call" | custom-call | tf_op jit(solution)/shard_map/total/pallas_call | solution.py:247
  25.5 3.9 %all-to-all-start.1 = ((f32[32,8,128]{2,1,0:T(8,128)}), f32[32,8,128]{2,1,0:T(8,128)S(1)}, u32[]{:S(2)}, u32[]{:S(2)}) async-start(f32[32,8,128]{2,1,0:T(8,128)} %get-tuple-element.8), calls=%async_computation.1 | async-start | bytes 262144 | tf_op jit(solution)/shard_map/all_to_all | solution.py:262
  29.4 2.8 %collective-permute-start.2 = (f32[1,128]{1,0:T(1,128)S(1)}, f32[1,128]{1,0:T(1,128)S(1)}, u32[]{:S(2)}, u32[]{:S(2)}) collective-permute-start(f32[1,128]{1,0:T(1,128)S(1)} %get-tuple-element.9.refs_3_), channel_id=1, source_target_pairs={{0,96},{32,0},{64,32},{96,64},{1,97},{33,1},{65,33},{97,65},{2,98}... | collective-permute-start | bytes 1544 | tf_op jit(solution)/shard_map/ppermute | solution.py:259
  32.2 0.3 collective-permute-start.1
  32.5 0.7 %collective-permute-start = (f32[1,128]{1,0:T(1,128)S(1)}, f32[1,128]{1,0:T(1,128)S(1)}, u32[]{:S(2)}, u32[]{:S(2)}) collective-permute-start(f32[1,128]{1,0:T(1,128)S(1)} %get-tuple-element.9.refs_3_), channel_id=1, source_target_pairs={{0,32},{32,64},{64,96},{96,0},{1,33},{33,65},{65,97},{97,1},{2,34}... | collective-permute-start | bytes 1544 | tf_op jit(solution)/shard_map/ppermute | solution.py:259
  33.3 0.0 collective-permute-done.2.refs_6_
  33.3 3.2 %collective-permute-done.1.refs_5_ = f32[1,128]{1,0:T(1,128)S(1)} collective-permute-done((f32[1,128]{1,0:T(1,128)S(1)}, f32[1,128]{1,0:T(1,128)S(1)}, u32[]{:S(2)}, u32[]{:S(2)}) %collective-permute-start.1) | collective-permute-done | bytes 544 | tf_op jit(solution)/shard_map/ppermute | solution.py:259
  36.4 0.0 collective-permute-done.refs_4_
  36.5 0.6 %all-to-all-done.1 = f32[32,8,128]{2,1,0:T(8,128)S(1)} async-done(((f32[32,8,128]{2,1,0:T(8,128)}), f32[32,8,128]{2,1,0:T(8,128)S(1)}, u32[]{:S(2)}, u32[]{:S(2)}) %all-to-all-start.1) | async-done | bytes 131104 | tf_op jit(solution)/shard_map/all_to_all | solution.py:262
  37.1 0.0 copy-done
  37.1 7.5 %finish.1 = (f32[2,8,8,64]{3,2,1,0:T(8,128)}, f32[8,8]{1,0:T(8,128)}, f32[2,8,3,8,1024]{4,3,2,1,0:T(8,128)}) custom-call(f32[4,64,128]{2,1,0:T(8,128)S(1)} %bitcast.6, f32[2,8,8,64]{3,2,1,0:T(8,128)S(1)} %bitcast.7, f32[2,8,3,64,1024]{4,3,2,1,0:T(8,128)} %bitcast.9, f32[1,128]{1,0:T(1,128)S(1)} %get-tuple-element.9.refs_3_, ...), custom_call_target="tpu_custom_call" | custom-call | tf_op jit(solution)/shard_map/finish/pallas_call | solution.py:264
Async XLA Ops:
  0.6 36.5 %copy-start = (f32[2,8,64,8]{2,3,1,0:T(8,128)S(1)}, f32[2,8,64,8]{2,3,1,0:T(8,128)}, u32[]{:S(2)}) copy-start(f32[2,8,64,8]{2,3,1,0:T(8,128)} %param.5) | copy-start | bytes 98308
  25.5 11.6 %all-to-all-start.1 = ((f32[32,8,128]{2,1,0:T(8,128)}), f32[32,8,128]{2,1,0:T(8,128)S(1)}, u32[]{:S(2)}, u32[]{:S(2)}) async-start(f32[32,8,128]{2,1,0:T(8,128)} %get-tuple-element.8), calls=%async_computation.1 | async-start | bytes 262144 | tf_op jit(solution)/shard_map/all_to_all | solution.py:262
  29.4 3.9 %collective-permute-start.2 = (f32[1,128]{1,0:T(1,128)S(1)}, f32[1,128]{1,0:T(1,128)S(1)}, u32[]{:S(2)}, u32[]{:S(2)}) collective-permute-start(f32[1,128]{1,0:T(1,128)S(1)} %get-tuple-element.9.refs_3_), channel_id=1, source_target_pairs={{0,96},{32,0},{64,32},{96,64},{1,97},{33,1},{65,33},{97,65},{2,98}... | collective-permute-start | bytes 1544 | tf_op jit(solution)/shard_map/ppermute | solution.py:259
  32.2 4.2 %collective-permute-start.1 = (f32[1,128]{1,0:T(1,128)S(1)}, f32[1,128]{1,0:T(1,128)S(1)}, u32[]{:S(2)}, u32[]{:S(2)}) collective-permute-start(f32[1,128]{1,0:T(1,128)S(1)} %get-tuple-element.9.refs_3_), channel_id=1, source_target_pairs={{0,64},{32,96},{64,0},{96,32},{1,65},{33,97},{65,1},{97,33},{2,66}... | collective-permute-start | bytes 1544 | tf_op jit(solution)/shard_map/ppermute | solution.py:259
  32.5 3.9 %collective-permute-start = (f32[1,128]{1,0:T(1,128)S(1)}, f32[1,128]{1,0:T(1,128)S(1)}, u32[]{:S(2)}, u32[]{:S(2)}) collective-permute-start(f32[1,128]{1,0:T(1,128)S(1)} %get-tuple-element.9.refs_3_), channel_id=1, source_target_pairs={{0,32},{32,64},{64,96},{96,0},{1,33},{33,65},{65,97},{97,1},{2,34}... | collective-permute-start | bytes 1544 | tf_op jit(solution)/shard_map/ppermute | solution.py:259

commit v4 on v2

--- a/solution.py
+++ b/solution.py
@@ -63,8 +63,8 @@
             trace = trace + jnp.where(row == col, real, 0.0)
         wide = jnp.concatenate(packed, axis=1)
         for b in range(blocks // 8):
-            start = (pair * (blocks // 8) + b) * 9
-            out[pl.ds(start, 8), 0, :] = wide[8 * b : 8 * b + 8, :]
+            for r in range(8):
+                out[pair * (blocks // 8) + b, :, both * r : both * (r + 1)] = wide[8 * b + r : 8 * b + r + 1, :]
         return trace
 
     def pair_step(pair, trace):
@@ -82,18 +82,18 @@
     value = jnp.sum(jnp.sum(trace, axis=1, keepdims=True), axis=0, keepdims=True)
     line = jnp.broadcast_to(value, (1, both))
     for piece in range(freqs // 2 * blocks // 8):
-        out[piece * 9 + 8, 0:1, :] = line
+        out[piece, :, 8 * both :] = line
 
 
 def sum_kernel(pieces, arrived, out, trace):
-    total = arrived[0:8, 0, :]
-    line = arrived[8, 0:1, :]
+    total = arrived[0]
     for p in range(1, pieces):
-        total = total + arrived[9 * p : 9 * p + 8, 0, :]
-        line = line + arrived[9 * p + 8, 0:1, :]
+        total = total + arrived[p]
+    width = out.shape[2]
+    lines = jnp.concatenate([total[:, width * r : width * (r + 1)] for r in range(8)], axis=0)
     for p in range(pieces):
-        out[p] = total
-    trace[...] = line
+        out[p] = lines
+    trace[...] = total[:, 8 * width :]
 
 
 def finish_kernel(freqs, blocks, comps, rank, groups, gram, basis, data, *refs):
@@ -220,7 +220,7 @@
     hbm = pl.BlockSpec(memory_space=pltpu.MemorySpace.HBM)
     packed = pl.pallas_call(
         lambda *refs: gram_kernel(freqs, blocks, comps, scaling, *refs),
-        out_shape=pltpu.VMEM((pieces * 9, 1, 2 * blocks), F32),
+        out_shape=pltpu.VMEM((pieces, 1, 18 * blocks), F32),
         in_specs=[hbm, hbm],
         out_specs=vmem,
         scratch_shapes=[

time: 44.9 us -> 44.9 us (level)
  no operation moved by 1% of the time
where the time goes in v4:
time: 44.9 us; the launch traced here: 44.7 us
  blocking collectives  17 us (38%)
  Pallas kernels  15.4 us (34%)
  starting transfers between devices  7.74 us (17%)
  waiting for transfers between devices  3.86 us (9%)
  between operations  0.66 us (1%)
    all_to_all x1, blocking collectives, per_device(): arrived = lax.all_to_all(packed, 'pts', 0, 0, tiled=True)  17 us
    pallas_call x1, Pallas kernels, per_device(): pl.pallas_call(lambda *refs: finish_kernel(freqs, blocks, comps, rank, fr...  7.55 us
    pallas_call x1, Pallas kernels, per_device(): pl.pallas_call(lambda *refs: gram_kernel(freqs, blocks, comps, scaling, *...  7.19 us
    all_to_all x1, starting transfers between devices, per_device(): lax.all_to_all(spread, 'pts', 0, 0, tiled=True)  3.9 us
    ppermute x3, starting transfers between devices, per_device(): lax.ppermute(trace, 'freq', [(i, (i + d) % freq_groups) for i in range(fr...  3.85 us
    ppermute x3, waiting for transfers between devices, per_device(): lax.ppermute(trace, 'freq', [(i, (i + d) % freq_groups) for i in range(fr...  3.23 us
  transfers between devices with their start and end apart: 4, of which 3 were waited for; matrix products, arithmetic and copies ran while one was open for 0% of the time, Pallas kernels for 0%

profile of v4, /device:TPU:1, one launch (start us, length us, event | category | flops | bytes accessed | tf_op | source)
XLA Modules:
  0.0 44.7 jit_solution(11109803319496352543)
XLA Ops:
  0.6 0.0 copy-start
  0.6 7.2 %gram.1 = f32[32,1,1152]{2,1,0:T(1,128)S(1)} custom-call(f32[2,8,3,64,1024]{4,3,2,1,0:T(8,128)} %bitcast.8, f32[1,1024]{1,0:T(1,128)} %bitcast.10), custom_call_target="tpu_custom_call" | custom-call | tf_op jit(solution)/shard_map/gram/pallas_call | solution.py:221
  7.8 17.0 %all_to_all.10.refs_0_ = f32[32,1,1152]{2,1,0:T(1,128)S(1)} all-to-all(f32[32,1,1152]{2,1,0:T(1,128)S(1)} %gram.1), channel_id=1, replica_groups=mesh['freq'=4,'pts'=32] {'pts'}, dimensions={0} | all-to-all | bytes 294912 | tf_op jit(solution)/shard_map/all_to_all | solution.py:235
  24.8 0.7 %total.1 = (f32[32,8,128]{2,1,0:T(8,128)}, f32[1,128]{1,0:T(1,128)S(1)}) custom-call(f32[32,1,1152]{2,1,0:T(1,128)S(1)} %all_to_all.10.refs_0_), custom_call_target="tpu_custom_call" | custom-call | tf_op jit(solution)/shard_map/total/pallas_call | solution.py:236
  25.5 3.9 %all-to-all-start.1 = ((f32[32,8,128]{2,1,0:T(8,128)}), f32[32,8,128]{2,1,0:T(8,128)S(1)}, u32[]{:S(2)}, u32[]{:S(2)}) async-start(f32[32,8,128]{2,1,0:T(8,128)} %get-tuple-element.8), calls=%async_computation.1 | async-start | bytes 262144 | tf_op jit(solution)/shard_map/all_to_all | solution.py:251
  29.4 2.8 %collective-permute-start.2 = (f32[1,128]{1,0:T(1,128)S(1)}, f32[1,128]{1,0:T(1,128)S(1)}, u32[]{:S(2)}, u32[]{:S(2)}) collective-permute-start(f32[1,128]{1,0:T(1,128)S(1)} %get-tuple-element.9.refs_3_), channel_id=1, source_target_pairs={{0,96},{32,0},{64,32},{96,64},{1,97},{33,1},{65,33},{97,65},{2,98}... | collective-permute-start | bytes 1544 | tf_op jit(solution)/shard_map/ppermute | solution.py:248
  32.2 0.3 collective-permute-start.1
  32.6 0.7 %collective-permute-start = (f32[1,128]{1,0:T(1,128)S(1)}, f32[1,128]{1,0:T(1,128)S(1)}, u32[]{:S(2)}, u32[]{:S(2)}) collective-permute-start(f32[1,128]{1,0:T(1,128)S(1)} %get-tuple-element.9.refs_3_), channel_id=1, source_target_pairs={{0,32},{32,64},{64,96},{96,0},{1,33},{33,65},{65,97},{97,1},{2,34}... | collective-permute-start | bytes 1544 | tf_op jit(solution)/shard_map/ppermute | solution.py:248
  33.3 0.0 collective-permute-done.2.refs_6_
  33.3 3.2 %collective-permute-done.1.refs_5_ = f32[1,128]{1,0:T(1,128)S(1)} collective-permute-done((f32[1,128]{1,0:T(1,128)S(1)}, f32[1,128]{1,0:T(1,128)S(1)}, u32[]{:S(2)}, u32[]{:S(2)}) %collective-permute-start.1) | collective-permute-done | bytes 544 | tf_op jit(solution)/shard_map/ppermute | solution.py:248
  36.4 0.1 collective-permute-done.refs_4_
  36.5 0.6 %all-to-all-done.1 = f32[32,8,128]{2,1,0:T(8,128)S(1)} async-done(((f32[32,8,128]{2,1,0:T(8,128)}), f32[32,8,128]{2,1,0:T(8,128)S(1)}, u32[]{:S(2)}, u32[]{:S(2)}) %all-to-all-start.1) | async-done | bytes 131104 | tf_op jit(solution)/shard_map/all_to_all | solution.py:251
  37.1 0.0 copy-done
  37.1 7.5 %finish.1 = (f32[2,8,8,64]{3,2,1,0:T(8,128)}, f32[8,8]{1,0:T(8,128)}, f32[2,8,3,8,1024]{4,3,2,1,0:T(8,128)}) custom-call(f32[4,64,128]{2,1,0:T(8,128)S(1)} %bitcast.6, f32[2,8,8,64]{3,2,1,0:T(8,128)S(1)} %bitcast.7, f32[2,8,3,64,1024]{4,3,2,1,0:T(8,128)} %bitcast.9, f32[1,128]{1,0:T(1,128)S(1)} %get-tuple-element.9.refs_3_, ...), custom_call_target="tpu_custom_call" | custom-call | tf_op jit(solution)/shard_map/finish/pallas_call | solution.py:253
Async XLA Ops:
  0.6 36.5 %copy-start = (f32[2,8,64,8]{2,3,1,0:T(8,128)S(1)}, f32[2,8,64,8]{2,3,1,0:T(8,128)}, u32[]{:S(2)}) copy-start(f32[2,8,64,8]{2,3,1,0:T(8,128)} %param.5) | copy-start | bytes 98308
  25.5 11.6 %all-to-all-start.1 = ((f32[32,8,128]{2,1,0:T(8,128)}), f32[32,8,128]{2,1,0:T(8,128)S(1)}, u32[]{:S(2)}, u32[]{:S(2)}) async-start(f32[32,8,128]{2,1,0:T(8,128)} %get-tuple-element.8), calls=%async_computation.1 | async-start | bytes 262144 | tf_op jit(solution)/shard_map/all_to_all | solution.py:251
  29.4 3.9 %collective-permute-start.2 = (f32[1,128]{1,0:T(1,128)S(1)}, f32[1,128]{1,0:T(1,128)S(1)}, u32[]{:S(2)}, u32[]{:S(2)}) collective-permute-start(f32[1,128]{1,0:T(1,128)S(1)} %get-tuple-element.9.refs_3_), channel_id=1, source_target_pairs={{0,96},{32,0},{64,32},{96,64},{1,97},{33,1},{65,33},{97,65},{2,98}... | collective-permute-start | bytes 1544 | tf_op jit(solution)/shard_map/ppermute | solution.py:248
  32.2 4.2 %collective-permute-start.1 = (f32[1,128]{1,0:T(1,128)S(1)}, f32[1,128]{1,0:T(1,128)S(1)}, u32[]{:S(2)}, u32[]{:S(2)}) collective-permute-start(f32[1,128]{1,0:T(1,128)S(1)} %get-tuple-element.9.refs_3_), channel_id=1, source_target_pairs={{0,64},{32,96},{64,0},{96,32},{1,65},{33,97},{65,1},{97,33},{2,66}... | collective-permute-start | bytes 1544 | tf_op jit(solution)/shard_map/ppermute | solution.py:248
  32.6 3.9 %collective-permute-start = (f32[1,128]{1,0:T(1,128)S(1)}, f32[1,128]{1,0:T(1,128)S(1)}, u32[]{:S(2)}, u32[]{:S(2)}) collective-permute-start(f32[1,128]{1,0:T(1,128)S(1)} %get-tuple-element.9.refs_3_), channel_id=1, source_target_pairs={{0,32},{32,64},{64,96},{96,0},{1,33},{33,65},{65,97},{97,1},{2,34}... | collective-permute-start | bytes 1544 | tf_op jit(solution)/shard_map/ppermute | solution.py:248
